TPU v7x, 512 devices: a whole 4x4x16 slice. The times are simulated.
512 devices in a mesh: row: 16 (over y, x), col: 32 (over z, core).
Axes of the slice: x: 4, y: 4, z: 16, core: 2. Of those that a mesh axis runs over, the one named last changes fastest.
Arguments:
- environment: bfloat16 [768, 16384], P(None, 'row'), may hold values from -6 to 6
- even_site: bfloat16 [16384, 2, 16384], P('row', None, 'col'), may hold values from -0.5 to 0.5
- odd_site: bfloat16 [16384, 2, 16384], P('col', None, 'row'), may hold values from -0.5 to 0.5
- outcomes: int32 [2, 768], replicated, may hold values from 0 to 1
- basis_codes: int32 [2, 768], replicated, may hold values from 0 to 1
Outputs:
- final_environment: bfloat16 [768, 16384], P('col', 'row')
- probabilities: float32 [2, 768], P(None, 'col')
Inputs may be any that keep to these rules, and one draw needn't show every extreme that they name: `outcomes`: outcome 0 or 1 of each measurement. `basis_codes`: 0 is the z basis, 1 the x basis.
All inputs are finite; a program needn't handle non-finite values.
Results may differ from a plain program's by a relative error of at most 0.028.
Values may be sent and summed in bfloat16 or wider, within the bound.
A program may use at most 64 MiB of HBM per device.

v0:
```python
import jax
import jax.numpy as jnp
from jax import lax
from jax.sharding import Mesh
from jax.sharding import PartitionSpec as P

CHI = 16384
COL = ("col_0", "col_1")


half_root = 0.7071067811865476


def split_up(x, dim, size):
    before, after = (x.shape[:dim], x.shape[dim + 1 :])
    return jnp.moveaxis(x.reshape(*before, size, -1, *after), dim, 0)


def sent_and_summed(x, axis, dim):
    parts = split_up(x, dim, lax.axis_size(axis))
    arrived = lax.all_to_all(parts, axis, split_axis=0, concat_axis=0, tiled=True)
    return arrived.astype(jnp.float32).sum(axis=0)


def copy_for_each(x, axis):
    copies = jnp.broadcast_to(x, (lax.axis_size(axis), *x.shape))
    return lax.all_to_all(copies, axis, split_axis=0, concat_axis=0, tiled=True)


def taken_together(x, axis):
    return copy_for_each(x, axis).sum(axis=0)


def joined_along(parts, dim):
    dims = list(parts.shape[1:])
    dims[dim] *= parts.shape[0]
    return jnp.moveaxis(parts, 0, dim).reshape(dims)


def gathered_copies(x, axis, dim):
    return joined_along(copy_for_each(x, axis), dim)


def sum_in_order(parts, axes, order):
    dims = [lax.axis_size(a) for a in axes]
    parts = parts.reshape(*dims, *parts.shape[1:])
    parts = parts.transpose(*order, *range(len(axes), parts.ndim))
    parts = parts.reshape(-1, *parts.shape[len(axes) :])
    for k in order:
        parts = lax.psum_scatter(parts, axes[k], scatter_dimension=0, tiled=True)
    return parts[0]


def summed_rows(x, axes, order, dim):
    size = lax.axis_size(axes)
    return sum_in_order(split_up(x, dim, size), axes, order)


def contract(vectors, tensor):
    left_size = tensor.shape[0]
    right_size = tensor.shape[2]
    product = jnp.dot(
        vectors, tensor.reshape(left_size, 2 * right_size), preferred_element_type=jnp.float32
    )
    return product.reshape(vectors.shape[0], 2, right_size)


def split_basis(summed, basis_row):
    upper = summed[:, 0, :]
    lower = summed[:, 1, :]
    rotate = (basis_row == 1)[:, None]
    first = jnp.where(rotate, (upper + lower) * half_root, upper)
    second = jnp.where(rotate, (upper - lower) * half_root, lower)
    return (first, second)


def local_squares(first, second):
    return jnp.stack([jnp.sum(first * first, axis=1), jnp.sum(second * second, axis=1)], axis=1)


def collapse(first, second, squares, outcome_row):
    pick = outcome_row == 1
    chosen = jnp.where(pick[:, None], second, first)
    chosen_norm = jnp.where(pick, squares[:, 1], squares[:, 0])
    return (chosen, chosen_norm, chosen_norm / (squares[:, 0] + squares[:, 1]))


def per_device(environment, even_site, odd_site, outcomes, basis_codes):
    samples_all = environment.shape[0]
    row_devices = lax.axis_size("row")
    col_devices = lax.axis_size(COL)
    row_place = lax.axis_index("row")
    col_place = lax.axis_index(COL)
    second_count = samples_all // col_devices
    second_start = col_place * second_count
    first_count = samples_all // row_devices
    first_start = row_place * first_count
    summed = sent_and_summed(contract(environment, even_site).astype(jnp.bfloat16), "row", 0)
    basis_first = lax.dynamic_slice_in_dim(basis_codes[0], first_start, first_count, 0)
    outcome_first = lax.dynamic_slice_in_dim(outcomes[0], first_start, first_count, 0)
    first, second = split_basis(summed, basis_first)
    squares = taken_together(local_squares(first, second), COL)
    chosen, chosen_norm, prob_first = collapse(first, second, squares, outcome_first)
    projected, prob_gathered = (
        gathered_copies(chosen.astype(jnp.bfloat16), "row", 0),
        gathered_copies(prob_first.astype(jnp.bfloat16), "row", 0).astype(prob_first.dtype),
    )
    summed = summed_rows(contract(projected, odd_site).astype(jnp.bfloat16), COL, (1, 0), 0).astype(
        jnp.float32
    )
    basis_second = lax.dynamic_slice_in_dim(basis_codes[1], second_start, second_count, 0)
    outcome_second = lax.dynamic_slice_in_dim(outcomes[1], second_start, second_count, 0)
    first, second = split_basis(summed, basis_second)
    squares = taken_together(local_squares(first, second), "row")
    chosen, chosen_norm, prob_second = collapse(first, second, squares, outcome_second)
    final_environment = (chosen * jnp.sqrt(CHI / chosen_norm)[:, None]).astype(jnp.bfloat16)
    probabilities = jnp.stack(
        [lax.dynamic_slice_in_dim(prob_gathered, second_start, second_count, 0), prob_second],
        axis=0,
    )
    return (final_environment, probabilities)


def solution(mesh):
    finer = Mesh(mesh.devices.reshape(mesh.shape["row"], 16, 2), ("row", "col_0", "col_1"))
    placed = (P(None, "row"), P("row", None, COL), P(COL, None, "row"), P(), P())
    return jax.shard_map(
        per_device,
        mesh=finer,
        in_specs=placed,
        out_specs=(P(COL, "row"), P(None, COL)),
        check_vma=False,
    )
```

profile of v0, /device:TPU:32, one launch (start us, length us, event | category | flops | bytes accessed | tf_op | source)
XLA Modules:
  0.0 215.4 jit_solution(11082512631757078441)
XLA Ops:
  7.2 3.6 %copy.16 = bf16[128,8,2,512]{3,1,2,0:T(8,128)(2,1)} copy(bf16[128,8,2,512]{3,2,1,0:T(2,128)(2,1)} %bitcast.132) | data formatting | bytes 4194304
  10.8 4.0 %copy.12 = bf16[1024,1024]{1,0:T(8,128)(2,1)} copy(bf16[1024,1024]{0,1:T(8,128)(2,1)} %bitcast.129) | data formatting | bytes 4194304 | tf_op jit(solution)/shard_map/dot_general | solution.py:62
  14.8 3.4 %convolution_convert_fusion.1 = bf16[768,2,512]{2,0,1:T(8,128)(2,1)S(1)} fusion(bf16[2,512,1024]{2,1,0:T(8,128)(2,1)} %bitcast.135, bf16[768,1024]{1,0:T(8,128)(2,1)S(1)} %copy-done), kind=kOutput, calls=%fused_computation.2 | convolution fusion | flops 1611399168 | bytes 5242880 | tf_op jit(solution)/shard_map/dot_general | solution.py:62
  18.2 1.3 copy.13
  19.4 7.2 %all-to-all-start = ((bf16[16,48,2,512]{3,1,2,0:T(8,128)(2,1)}), bf16[16,48,2,512]{3,1,2,0:T(8,128)(2,1)S(1)}, u32[]{:S(2)}, u32[]{:S(2)}) async-start(bf16[16,48,2,512]{3,1,2,0:T(8,128)(2,1)} %copy.13), calls=%async_computation | async-start | bytes 3145728 | tf_op jit(solution)/shard_map/all_to_all | solution.py:21
  26.6 0.1 compare_bitcast_fusion
  26.7 24.4 %all-to-all-done = bf16[16,48,2,512]{3,1,2,0:T(8,128)(2,1)S(1)} async-done(((bf16[16,48,2,512]{3,1,2,0:T(8,128)(2,1)}), bf16[16,48,2,512]{3,1,2,0:T(8,128)(2,1)S(1)}, u32[]{:S(2)}, u32[]{:S(2)}) %all-to-all-start) | async-done | bytes 1572896 | tf_op jit(solution)/shard_map/all_to_all | solution.py:21
  51.1 0.2 convert_reduce_fusion
  51.4 0.2 multiply_reduce_fusion.1
  51.6 0.6 broadcast_in_dim.55
  52.2 15.4 %all-to-all-start.3 = ((f32[32,48,2]{1,2,0:T(2,128)}), f32[32,48,2]{1,2,0:T(2,128)S(1)}, u32[]{:S(2)}, u32[]{:S(2)}) async-start(f32[32,48,2]{1,2,0:T(2,128)} %broadcast_in_dim.55), calls=%async_computation.5 | async-start | bytes 65536 | tf_op jit(solution)/shard_map/all_to_all | solution.py:27
  67.6 11.7 %all-to-all-done.3 = f32[32,48,2]{1,2,0:T(2,128)S(1)} async-done(((f32[32,48,2]{1,2,0:T(2,128)}), f32[32,48,2]{1,2,0:T(2,128)S(1)}, u32[]{:S(2)}, u32[]{:S(2)}) %all-to-all-start.3) | async-done | bytes 12320 | tf_op jit(solution)/shard_map/all_to_all | solution.py:27
  79.4 0.1 select_convert_fusion
  79.5 1.0 broadcast_in_dim.53
  80.5 3.6 %all-to-all-start.1 = ((bf16[16,48,512]{2,1,0:T(8,128)(2,1)}), bf16[16,48,512]{2,1,0:T(8,128)(2,1)S(1)}, u32[]{:S(2)}, u32[]{:S(2)}) async-start(bf16[16,48,512]{2,1,0:T(8,128)(2,1)} %broadcast_in_dim.53), calls=%async_computation.1 | async-start | bytes 1572864 | tf_op jit(solution)/shard_map/all_to_all | solution.py:27
  84.2 3.5 %copy.17 = bf16[64,8,2,1024]{3,1,2,0:T(8,128)(2,1)} copy(bf16[64,8,2,1024]{3,2,1,0:T(2,128)(2,1)} %bitcast.133) | data formatting | bytes 4194304
  87.6 3.9 %copy.14 = bf16[2048,512]{1,0:T(8,128)(2,1)} copy(bf16[2048,512]{0,1:T(8,128)(2,1)} %bitcast.130) | data formatting | bytes 4194304 | tf_op jit(solution)/shard_map/dot_general | solution.py:62
  91.6 6.7 %all-to-all-done.1 = bf16[16,48,512]{2,1,0:T(8,128)(2,1)S(1)} async-done(((bf16[16,48,512]{2,1,0:T(8,128)(2,1)}), bf16[16,48,512]{2,1,0:T(8,128)(2,1)S(1)}, u32[]{:S(2)}, u32[]{:S(2)}) %all-to-all-start.1) | async-done | bytes 786464 | tf_op jit(solution)/shard_map/all_to_all | solution.py:27
  98.3 3.4 %convolution_convert_fusion = bf16[768,2,1024]{2,0,1:T(8,128)(2,1)S(1)} fusion(bf16[768,512,1]{1,0,2:T(8,128)(2,1)S(1)} %bitcast.137, bf16[2,1024,512]{2,1,0:T(8,128)(2,1)} %bitcast.134), kind=kOutput, calls=%fused_computation.1 | convolution fusion | flops 1612185600 | bytes 6029312 | tf_op jit(solution)/shard_map/dot_general | solution.py:62
  101.7 2.1 copy.15
  103.9 10.8 %reduce-scatter.3.cloned.1.call-done = bf16[16,24,2,1024]{3,1,2,0:T(8,128)(2,1)} async-done(((bf16[32,24,2,1024]{3,1,2,0:T(8,128)(2,1)}), bf16[16,24,2,1024]{3,1,2,0:T(8,128)(2,1)}) %reduce-scatter.3.cloned.1.call-update) | async-done | bytes 1572880 | tf_op jit(solution)/shard_map/reduce_scatter | solution.py:50
  114.9 0.6 broadcast_in_dim.56
  115.5 6.8 %all-to-all-start.4 = ((bf16[16,1,48]{2,1,0:T(2,128)(2,1)}), bf16[16,1,48]{2,1,0:T(2,128)(2,1)S(1)}, u32[]{:S(2)}, u32[]{:S(2)}) async-start(bf16[16,1,48]{2,1,0:T(2,128)(2,1)} %broadcast_in_dim.56), calls=%async_computation.6 | async-start | bytes 16384 | tf_op jit(solution)/shard_map/all_to_all | solution.py:27
  122.4 7.4 %all-to-all-done.4 = bf16[16,1,48]{2,1,0:T(2,128)(2,1)S(1)} async-done(((bf16[16,1,48]{2,1,0:T(2,128)(2,1)}), bf16[16,1,48]{2,1,0:T(2,128)(2,1)S(1)}, u32[]{:S(2)}, u32[]{:S(2)}) %all-to-all-start.4) | async-done | bytes 1568 | tf_op jit(solution)/shard_map/all_to_all | solution.py:27
  129.9 61.0 %reduce-scatter.5.cloned.1.call-done = bf16[1,24,2,1024]{3,1,2,0:T(8,128)(2,1)} async-done(((bf16[16,24,2,1024]{3,1,2,0:T(8,128)(2,1)}), bf16[1,24,2,1024]{3,1,2,0:T(8,128)(2,1)}) %reduce-scatter.5.cloned.1.call-update) | async-done | bytes 98320 | tf_op jit(solution)/shard_map/reduce_scatter | solution.py:50
  191.0 0.9 bitcast_convert_fusion
  191.9 0.2 multiply_reduce_fusion.3
  192.1 0.6 broadcast_in_dim.54
  192.7 6.8 %all-to-all-start.2 = ((f32[16,24,2]{1,2,0:T(2,128)}), f32[16,24,2]{1,2,0:T(2,128)S(1)}, u32[]{:S(2)}, u32[]{:S(2)}) async-start(f32[16,24,2]{1,2,0:T(2,128)} %broadcast_in_dim.54), calls=%async_computation.4 | async-start | bytes 32768 | tf_op jit(solution)/shard_map/all_to_all | solution.py:27
  199.6 7.5 %all-to-all-done.2 = f32[16,24,2]{1,2,0:T(2,128)S(1)} async-done(((f32[16,24,2]{1,2,0:T(2,128)}), f32[16,24,2]{1,2,0:T(2,128)S(1)}, u32[]{:S(2)}, u32[]{:S(2)}) %all-to-all-start.2) | async-done | bytes 3104 | tf_op jit(solution)/shard_map/all_to_all | solution.py:27
  207.3 0.7 multiply_convert_fusion
  208.0 0.6 pad_maximum_fusion.2
  (24 shorter events, 0.8 us)
Async XLA Ops:
  7.2 7.6 %copy-start = (bf16[768,1024]{1,0:T(8,128)(2,1)S(1)}, bf16[768,1024]{1,0:T(8,128)(2,1)}, u32[]{:S(2)}) copy-start(bf16[768,1024]{1,0:T(8,128)(2,1)} %param.5) | copy-start | bytes 4718596
  19.4 7.2 %copy-start.1 = (s32[2,768]{1,0:T(2,128)S(1)}, s32[2,768]{1,0:T(2,128)}, u32[]{:S(2)}) copy-start(s32[2,768]{1,0:T(2,128)} %param.9) | copy-start | bytes 18436
  19.4 48.1 %copy-start.2 = (s32[2,768]{1,0:T(2,128)S(1)}, s32[2,768]{1,0:T(2,128)}, u32[]{:S(2)}) copy-start(s32[2,768]{1,0:T(2,128)} %param.8) | copy-start | bytes 18436
  19.4 31.7 %all-to-all-start = ((bf16[16,48,2,512]{3,1,2,0:T(8,128)(2,1)}), bf16[16,48,2,512]{3,1,2,0:T(8,128)(2,1)S(1)}, u32[]{:S(2)}, u32[]{:S(2)}) async-start(bf16[16,48,2,512]{3,1,2,0:T(8,128)(2,1)} %copy.13), calls=%async_computation | async-start | bytes 3145728 | tf_op jit(solution)/shard_map/all_to_all | solution.py:21
  52.2 27.1 %all-to-all-start.3 = ((f32[32,48,2]{1,2,0:T(2,128)}), f32[32,48,2]{1,2,0:T(2,128)S(1)}, u32[]{:S(2)}, u32[]{:S(2)}) async-start(f32[32,48,2]{1,2,0:T(2,128)} %broadcast_in_dim.55), calls=%async_computation.5 | async-start | bytes 65536 | tf_op jit(solution)/shard_map/all_to_all | solution.py:27
  80.5 17.8 %all-to-all-start.1 = ((bf16[16,48,512]{2,1,0:T(8,128)(2,1)}), bf16[16,48,512]{2,1,0:T(8,128)(2,1)S(1)}, u32[]{:S(2)}, u32[]{:S(2)}) async-start(bf16[16,48,512]{2,1,0:T(8,128)(2,1)} %broadcast_in_dim.53), calls=%async_computation.1 | async-start | bytes 1572864 | tf_op jit(solution)/shard_map/all_to_all | solution.py:27
  84.1 30.6 %reduce-scatter.3.cloned.1.call-start = ((), (), s32[]{:S(2)}) async-start(), calls=%async_computation.7 | async-start | bytes 4718592 | tf_op jit(solution)/shard_map/reduce_scatter | solution.py:50
  103.9 87.1 %reduce-scatter.5.cloned.1.call-start = ((), (), s32[]{:S(2)}) async-start(), calls=%async_computation.8 | async-start | bytes 1671168 | tf_op jit(solution)/shard_map/reduce_scatter | solution.py:50
  115.5 14.3 %all-to-all-start.4 = ((bf16[16,1,48]{2,1,0:T(2,128)(2,1)}), bf16[16,1,48]{2,1,0:T(2,128)(2,1)S(1)}, u32[]{:S(2)}, u32[]{:S(2)}) async-start(bf16[16,1,48]{2,1,0:T(2,128)(2,1)} %broadcast_in_dim.56), calls=%async_computation.6 | async-start | bytes 16384 | tf_op jit(solution)/shard_map/all_to_all | solution.py:27
  192.7 14.4 %all-to-all-start.2 = ((f32[16,24,2]{1,2,0:T(2,128)}), f32[16,24,2]{1,2,0:T(2,128)S(1)}, u32[]{:S(2)}, u32[]{:S(2)}) async-start(f32[16,24,2]{1,2,0:T(2,128)} %broadcast_in_dim.54), calls=%async_computation.4 | async-start | bytes 32768 | tf_op jit(solution)/shard_map/all_to_all | solution.py:27
Sparse Core Ops, SparseCore 0:
  104.0 10.7 reduce-scatter.2
  117.6 73.3 reduce-scatter.4
where the time goes:
time: 216 us; the launch traced here: 215 us
  waiting for transfers between devices  130 us (60%)
  starting transfers between devices  39.9 us (18%)
  local copies, waits for them, and re-layouts  21.4 us (10%)
  between operations  14.2 us (7%)
  matrix products  6.83 us (3%)
  other arithmetic  3.5 us (2%)
    reduce_scatter x2, waiting for transfers between devices, sum_in_order(): parts = lax.psum_scatter(parts, axes[k], scatter_dimension=0, tiled=True)  71.9 us
    all_to_all x4, waiting for transfers between devices, copy_for_each(): return lax.all_to_all(copies, axis, split_axis=0, concat_axis=0, tiled=True)  33.4 us
    all_to_all x4, starting transfers between devices, copy_for_each(): return lax.all_to_all(copies, axis, split_axis=0, concat_axis=0, tiled=True)  32.6 us
    all_to_all x1, waiting for transfers between devices, sent_and_summed(): lax.all_to_all(parts, axis, split_axis=0, concat_axis=0, tiled=True)  24.4 us
    dot_general x2, local copies, waits for them, and re-layouts, contract(): jnp.dot(vectors, tensor.reshape(left_size, 2 * right_size), preferred_ele...  7.89 us
    all_to_all x1, starting transfers between devices, sent_and_summed(): lax.all_to_all(parts, axis, split_axis=0, concat_axis=0, tiled=True)  7.16 us
    unnamed x8, local copies, waits for them, and re-layouts  7.13 us
    dot_general x2, matrix products, contract(): jnp.dot(vectors, tensor.reshape(left_size, 2 * right_size), preferred_ele...  6.83 us
  transfers between devices with their start and end apart: 7, of which 7 were waited for; matrix products, arithmetic and copies ran while one was open for 4% of the time, Pallas kernels for 0%

commit v1 on v0

v1 whole, which is shorter than its diff:
```python
import jax
import jax.numpy as jnp
from jax import lax
from jax.experimental import pallas as pl
from jax.experimental.pallas import tpu as pltpu
from jax.sharding import PartitionSpec as P

CHI = 16384
HALF_ROOT = 0.7071067811865476
F32 = jnp.float32
BF16 = jnp.bfloat16
MESH = pl.DeviceIdType.MESH

NA = 4
NZ = 16
G = NA * NA
HZ = NZ // 2
GROUP = 24
NB = 3
SB = GROUP // NB
R = 2 * SB
COLS = 512
RIGHT = 1024


def coefficients(sel):
    rotated = sel >= 1.5
    odd = (sel == 1.0) | (sel == 3.0)
    sign = jnp.where(odd, -HALF_ROOT, HALF_ROOT)
    a = jnp.where(rotated, HALF_ROOT, jnp.where(odd, 0.0, 1.0))
    b = jnp.where(rotated, sign, jnp.where(odd, 1.0, 0.0))
    c = jnp.where(rotated, HALF_ROOT, jnp.where(odd, 1.0, 0.0))
    d = jnp.where(rotated, -sign, jnp.where(odd, 0.0, 1.0))
    return ((a, b), (c, d))


def kernel(
    env_hbm,
    te_hbm,
    to_hbm,
    outcomes,
    basis,
    out_ref,
    prob_ref,
    env_v,
    te_v,
    to_v,
    flat,
    w0,
    acc0,
    sel,
    s1,
    r1,
    s2,
    r2,
    g_buf,
    lhs,
    tb,
    acc1,
    part,
    zs,
    zr,
    fin,
    msg,
    n0r,
    nfs,
    nfr,
    load_sem,
    s1_sem,
    r1_sem,
    s2_sem,
    r2_sem,
    ga_ssem,
    ga_rsem,
    gb_ssem,
    gb_rsem,
    tb_ssem,
    tb_rsem,
    z_ssem,
    z_rsem,
    n0_ssem,
    n0_rsem,
    nf_ssem,
    nf_rsem,
):
    row = lax.axis_index("row")
    col = lax.axis_index("col")
    z = col // 2
    core = col % 2
    x = row % NA
    y = row // NA
    first_place = (x, y)
    second_place = (y, x)

    def at(px, py, pz, pc):
        return {"row": py * NA + px, "col": pz * 2 + pc}

    def peer(f, a, b, pc):
        return at(a, b, z, pc) if f == 0 else at(b, a, z, pc)

    def send(src, dst, ssem, rsem, device):
        pltpu.make_async_remote_copy(
            src_ref=src, dst_ref=dst, send_sem=ssem, recv_sem=rsem, device_id=device, device_id_type=MESH
        ).start()

    def wait_bytes(ref, sem):
        pltpu.make_async_copy(ref, ref, sem).wait()

    loads = [
        pltpu.make_async_copy(te_hbm, te_v, load_sem.at[0]),
        pltpu.make_async_copy(env_hbm, env_v, load_sem.at[1]),
        pltpu.make_async_copy(to_hbm, to_v, load_sem.at[2]),
    ]
    for load in loads:
        load.start()

    barrier = pltpu.get_barrier_semaphore()

    def hello(device):
        pl.semaphore_signal(barrier, inc=1, device_id=device, device_id_type=MESH)

    for dx in range(NA):
        for dy in range(NA):
            for dc in range(2):
                if dx == 0 and dy == 0 and dc == 0:
                    continue
                if dc == 1 and dx != 0 and dy != 0:
                    continue
                hello(at((x + dx) % NA, (y + dy) % NA, z, (core + dc) % 2))
    for dz in range(1, NZ):
        hello(at(x, y, (z + dz) % NZ, core))

    eye = lax.broadcasted_iota(jnp.int32, (128, 128), 0) == lax.broadcasted_iota(jnp.int32, (128, 128), 1)
    for s in range(2):
        for j in range(6):
            lanes = slice(j * 128, (j + 1) * 128)
            code = (2 * basis[s : s + 1, lanes] + outcomes[s : s + 1, lanes]).astype(F32)
            column = jnp.sum(jnp.where(eye, jnp.broadcast_to(code, (128, 128)), 0.0), axis=1, keepdims=True)
            sel[s, j * 128 : (j + 1) * 128, :] = jnp.broadcast_to(column, (128, 128))

    loads[0].wait()

    def spread_even(i, carry):
        l0 = pl.multiple_of(i * 128, 128)
        flat[0:1024, :] = te_v[pl.ds(l0, 128)].astype(F32).reshape(1024, 128)
        for lt in range(4):
            for s in range(2):
                w0[pl.ds(l0, 128), s * COLS + lt * 128 : s * COLS + lt * 128 + 128] = flat[
                    pl.ds(lt * 2 + s, 128, stride=8), :
                ].astype(BF16)
        return carry

    lax.fori_loop(0, 8, spread_even, 0)
    loads[1].wait()

    def multiply_first(i, carry):
        m0 = pl.multiple_of(i * 256, 256)
        rows = env_v[pl.ds(i * 32, 32)].reshape(256, 1024)
        for n in range(2):
            acc0[pl.ds(m0, 256), n * 512 : n * 512 + 512] = jnp.dot(
                rows, w0[:, n * 512 : n * 512 + 512], preferred_element_type=F32
            )
        return carry

    lax.fori_loop(0, 3, multiply_first, 0)

    def build_first(k, v):
        def one(gp, carry):
            g = gp // 2
            p = gp % 2
            gx = g % NA
            gy = g // NA
            rows = pl.ds(pl.multiple_of(gp * GROUP + k * SB, 8), SB)
            cu, cd = coefficients(sel[0, rows, :])[v]
            for f in range(2):
                halves = []
                for h in range(2):
                    lo = h * 256 + f * 128
                    halves.append(cu * acc0[rows, lo : lo + 128] + cd * acc0[rows, COLS + lo : COLS + lo + 128])
                ga, gb = (gx, gy) if f == 0 else (gy, gx)
                s1[k, v, f, p, ga, gb] = jnp.concatenate(halves, axis=0).astype(BF16)
            return carry

        lax.fori_loop(0, 2 * G, one, 0)

    def send_first(k, v):
        for da in (2, 1, 3, 0):
            for f in range(2):
                a = (first_place[f] + da) % NA
                for dc in range(2):
                    if da == 0 and dc == 0:
                        continue
                    pc = (core + dc) % 2
                    send(
                        s1.at[k, v, f, pc, a],
                        r1.at[k, v, f, first_place[f] * 2 + core],
                        s1_sem,
                        r1_sem.at[k, v, f],
                        peer(f, a, second_place[f], pc),
                    )

    def reduce_first(k, v):
        for f in range(2):
            r1[k, v, f, first_place[f] * 2 + core] = s1[k, v, f, core, first_place[f]]
            wait_bytes(r1.at[k, v, f, 0:7], r1_sem.at[k, v, f])
            for b in range(NA):
                for c in range(2):
                    total = r1[k, v, f, c, b].astype(F32)
                    for a in range(1, NA):
                        total = total + r1[k, v, f, a * 2 + c, b].astype(F32)
                    s2[k, v, f, b, c] = total.astype(BF16)
            for db in (2, 1, 3):
                b = (second_place[f] + db) % NA
                send(
                    s2.at[k, v, f, b],
                    r2.at[k, v, f, second_place[f]],
                    s2_sem,
                    r2_sem.at[k, v, f],
                    peer(f, first_place[f], b, core),
                )

    lane = lax.broadcasted_iota(jnp.int32, (SB, 128), 1)
    sub = lax.broadcasted_iota(jnp.int32, (SB, 128), 0)

    def norms_to_lanes(squares, base):
        sums = jnp.sum(squares, axis=1, keepdims=True)
        column = sums[:SB] + sums[SB:]
        return jnp.sum(jnp.where(lane == sub + base, column, 0.0), axis=0, keepdims=True)

    def finish_first(k, v):
        squares = jnp.zeros((R, 128), F32)
        for f in range(2):
            r2[k, v, f, second_place[f]] = s2[k, v, f, second_place[f]]
            wait_bytes(r2.at[k, v, f, 0:3], r2_sem.at[k, v, f])
            for c in range(2):
                total = r2[k, v, f, 0, c].astype(F32)
                for b in range(1, NA):
                    total = total + r2[k, v, f, b, c].astype(F32)
                squares = squares + total * total
                if v == 0:
                    g_buf[k, f, first_place[f], second_place[f], c] = total.astype(BF16)
            if v == 0:
                for db in (2, 1, 3):
                    b = (second_place[f] + db) % NA
                    here = g_buf.at[k, f, first_place[f], second_place[f]]
                    send(here, here, ga_ssem, ga_rsem.at[k, f], peer(f, first_place[f], b, core))
        msg[0:1, :] += norms_to_lanes(squares, 64 + 32 * v + k * SB)

    def pass_on(k):
        for f in range(2):
            wait_bytes(g_buf.at[k, f, 0, 0:3], ga_rsem.at[k, f])
            for da in (2, 1, 3):
                a = (first_place[f] + da) % NA
                here = g_buf.at[k, f, first_place[f]]
                send(here, here, gb_ssem, gb_rsem.at[k, f], peer(f, a, second_place[f], core))

    def multiply_second(k):
        for f in range(2):
            wait_bytes(g_buf.at[k, f, 0:3], gb_rsem.at[k, f])

        def pair(j, carry):
            m0 = pl.multiple_of(j * 2 * SB, 2 * SB)
            gy = j // 2
            for f in range(2):
                for c in range(2):
                    two = []
                    for e in range(2):
                        gx = (2 * j + e) % NA
                        ga, gb = (gx, gy) if f == 0 else (gy, gx)
                        two.append(g_buf[k, f, ga, gb, c].astype(F32))
                    for h in range(2):
                        lo = h * 512 + c * 256 + f * 128
                        lhs[pl.ds(m0, 2 * SB), lo : lo + 128] = jnp.concatenate(
                            [t[h * SB : (h + 1) * SB] for t in two], axis=0
                        ).astype(BF16)
            return carry

        lax.fori_loop(0, G // 2, pair, 0)
        left = lhs[...]

        def columns(n, carry):
            cols = pl.ds(pl.multiple_of(n * 256, 256), 256)
            acc1[:, cols] = jnp.dot(left, tb[:, :, :, cols].reshape(1024, 256), preferred_element_type=F32)
            return carry

        lax.fori_loop(0, 8, columns, 0)

        def one(g, carry):
            rows = pl.ds(pl.multiple_of(g * SB, 8), SB)
            samples = pl.ds(pl.multiple_of((2 * g + core) * GROUP + k * SB, 8), SB)
            pairs = coefficients(sel[1, samples, :])
            for v in range(2):
                cu, cd = pairs[v]
                for t in range(4):
                    halves = []
                    for h in range(2):
                        lo = h * 512 + t * 128
                        halves.append(
                            cu * acc1[rows, lo : lo + 128] + cd * acc1[rows, RIGHT + lo : RIGHT + lo + 128]
                        )
                    part[k, v, g, :, t * 128 : t * 128 + 128] = jnp.concatenate(halves, axis=0).astype(BF16)
            return carry

        lax.fori_loop(0, G, one, 0)

    def hops(v, d):
        return HZ - v if d == 0 else HZ - 1 + v

    def slot(v, d, s):
        return {(0, 0): 0, (0, 1): HZ, (1, 0): 2 * HZ - 1, (1, 1): 3 * HZ - 2}[v, d] + s

    def ring_step(k, s):
        for v in range(2):
            for d in range(2):
                n = hops(v, d)
                if s >= n:
                    continue
                owner = (z + n - s) % NZ if d == 0 else (z + NZ - n + s) % NZ
                step = 1 if d == 0 else NZ - 1
                here = slot(v, d, s)
                if s == 0:
                    src = part.at[k, v, owner]
                else:
                    wait_bytes(zr.at[k, here - 1], z_rsem.at[k, here - 1])
                    zs[k, here] = (zr[k, here - 1].astype(F32) + part[k, v, owner].astype(F32)).astype(BF16)
                    src = zs.at[k, here]
                send(src, zr.at[k, here], z_ssem, z_rsem.at[k, here], at(x, y, (z + step) % NZ, core))

    def ring_end(k):
        for v in range(2):
            total = part[k, v, z].astype(F32)
            for d in range(2):
                last = slot(v, d, hops(v, d) - 1)
                wait_bytes(zr.at[k, last], z_rsem.at[k, last])
                total = total + zr[k, last].astype(F32)
            if v == 0:
                fin[k * SB : (k + 1) * SB, 0:512] = total[:SB]
                fin[k * SB : (k + 1) * SB, 512:1024] = total[SB:]
            msg[1:2, :] += norms_to_lanes(total * total, 32 * v + k * SB)

    msg[...] = jnp.zeros_like(msg)
    pl.semaphore_wait(barrier, 37)

    for k in range(NB):
        build_first(k, 0)
        send_first(k, 0)

    loads[2].wait()

    def spread_odd(i, carry):
        flat[...] = to_v[pl.ds(i * 256, 256)].astype(F32).reshape(2048, 128)
        h = i // 2
        w = pl.multiple_of((i % 2) * 128, 128)
        for lt in range(8):
            for s in range(2):
                lo = s * RIGHT + lt * 128
                tb[h, core, pl.ds(w, 128), lo : lo + 128] = flat[pl.ds(lt * 2 + s, 128, stride=16), :].astype(BF16)
        return carry

    lax.fori_loop(0, 4, spread_odd, 0)
    for h in range(2):
        send(tb.at[h, core], tb.at[h, core], tb_ssem, tb_rsem, at(x, y, z, 1 - core))
    for k in range(NB):
        build_first(k, 1)

    for k in range(NB):
        reduce_first(k, 0)
    for k in range(NB):
        finish_first(k, 0)
    for k in range(NB):
        pass_on(k)
    for k in range(NB):
        send_first(k, 1)
    wait_bytes(tb.at[:, 0], tb_rsem)

    for tick in range(HZ + NB):
        if tick < NB:
            multiply_second(tick)
        for k in range(NB - 1, -1, -1):
            s = tick - k
            if 0 <= s < HZ:
                ring_step(k, s)
            elif s == HZ:
                ring_end(k)
        if tick == NB:
            for k in range(NB):
                reduce_first(k, 1)
        if tick == NB + 2:
            for k in range(NB):
                finish_first(k, 1)
            n0r[z] = msg[0:1, :]
            nfs[0:1, :] = msg[0:1, :]

            @pl.when(z != row)
            def _():
                send(nfs.at[0:1], n0r.at[z], n0_ssem, n0_rsem, at(x, y, row, core))

    nfs[1:2, :] = msg[1:2, :]

    @pl.when(z == row)
    def _():
        wait_bytes(n0r.at[0 : NZ - 1], n0_rsem)
        nfs[1:2, :] = msg[1:2, :] + jnp.sum(n0r[...], axis=0)

    nfr[row] = nfs[1:2, :]
    for dx in range(NA):
        for dy in range(NA):
            if dx or dy:
                send(nfs.at[1:2], nfr.at[row], nf_ssem, nf_rsem, at((x + dx) % NA, (y + dy) % NA, z, core))
    wait_bytes(nfr.at[0 : G - 1], nf_rsem)
    norms = jnp.sum(nfr[...], axis=0)
    prob = norms / (norms + pltpu.roll(norms, 96, 1))
    prob_ref[0:1, :] = pltpu.roll(prob, 64, 1)[:, :GROUP]
    prob_ref[1:2, :] = prob[:, :GROUP]
    lane24 = lax.broadcasted_iota(jnp.int32, (GROUP, 128), 1)
    sub24 = lax.broadcasted_iota(jnp.int32, (GROUP, 128), 0)
    column = jnp.sum(jnp.where(lane24 == sub24, jnp.broadcast_to(norms, (GROUP, 128)), 0.0), axis=1, keepdims=True)
    out_ref[...] = (fin[...] * jnp.sqrt(CHI / column)).astype(BF16)

    wait_bytes(r1.at[:, :, :, 0:7], s1_sem)
    wait_bytes(r2.at[:, :, :, 0:3], s2_sem)
    wait_bytes(g_buf.at[:, :, 0, 0:3], ga_ssem)
    wait_bytes(g_buf.at[:, :, 0:3], gb_ssem)
    wait_bytes(tb.at[:, 0], tb_ssem)
    wait_bytes(zr, z_ssem)

    @pl.when(z != row)
    def _():
        wait_bytes(n0r.at[0], n0_ssem)

    wait_bytes(nfr.at[0 : G - 1], nf_ssem)


def per_device(environment, even_site, odd_site, outcomes, basis_codes):
    samples, left = environment.shape
    env = environment.reshape(samples // 8, 8, left)
    te = even_site.reshape(left, 2, 4, 128).transpose(0, 2, 1, 3).reshape(left, 8, 128)
    to = odd_site.reshape(512, 2, 8, 128).transpose(0, 2, 1, 3).reshape(1024, 8, 128)
    vmem = pl.BlockSpec(memory_space=pltpu.VMEM)
    hbm = pl.BlockSpec(memory_space=pl.ANY)
    dma = pltpu.SemaphoreType.DMA
    nz_slots = 4 * HZ - 2
    return pl.pallas_call(
        kernel,
        out_shape=(
            jax.ShapeDtypeStruct((GROUP, RIGHT), BF16),
            jax.ShapeDtypeStruct((2, GROUP), F32),
        ),
        in_specs=[hbm, hbm, hbm, vmem, vmem],
        out_specs=(vmem, vmem),
        scratch_shapes=[
            pltpu.VMEM((samples // 8, 8, left), BF16),
            pltpu.VMEM((left, 8, 128), BF16),
            pltpu.VMEM((1024, 8, 128), BF16),
            pltpu.VMEM((2048, 128), F32),
            pltpu.VMEM((left, 2 * COLS), BF16),
            pltpu.VMEM((samples, 2 * COLS), F32),
            pltpu.VMEM((2, samples, 128), F32),
            pltpu.VMEM((NB, 2, 2, 2, NA, NA, R, 128), BF16),
            pltpu.VMEM((NB, 2, 2, 2 * NA, NA, R, 128), BF16),
            pltpu.VMEM((NB, 2, 2, NA, 2, R, 128), BF16),
            pltpu.VMEM((NB, 2, 2, NA, 2, R, 128), BF16),
            pltpu.VMEM((NB, 2, NA, NA, 2, R, 128), BF16),
            pltpu.VMEM((G * SB, 1024), BF16),
            pltpu.VMEM((2, 2, 256, 2 * RIGHT), BF16),
            pltpu.VMEM((G * SB, 2 * RIGHT), F32),
            pltpu.VMEM((NB, 2, NZ, R, 512), BF16),
            pltpu.VMEM((NB, nz_slots, R, 512), BF16),
            pltpu.VMEM((NB, nz_slots, R, 512), BF16),
            pltpu.VMEM((GROUP, RIGHT), F32),
            pltpu.VMEM((8, 128), F32),
            pltpu.VMEM((NZ, 1, 128), F32),
            pltpu.VMEM((8, 128), F32),
            pltpu.VMEM((G, 1, 128), F32),
            dma((3,)),
            dma,
            dma((NB, 2, 2)),
            dma,
            dma((NB, 2, 2)),
            dma,
            dma((NB, 2)),
            dma,
            dma((NB, 2)),
            dma,
            dma,
            dma,
            dma((NB, nz_slots)),
            dma,
            dma,
            dma,
            dma,
        ],
        compiler_params=pltpu.CompilerParams(
            collective_id=0, has_side_effects=True, vmem_limit_bytes=60 * 1024 * 1024
        ),
    )(env, te, to, outcomes, basis_codes)


def solution(mesh):
    placed = (P(None, "row"), P("row", None, "col"), P("col", None, "row"), P(), P())
    return jax.shard_map(
        per_device,
        mesh=mesh,
        in_specs=placed,
        out_specs=(P("col", "row"), P(None, "col")),
        check_vma=False,
    )
```

time: 216 us -> 77.2 us (0.36)
  the two profiles are of different devices: /device:TPU:32 before, /device:TPU:8 now
where the time goes in v1:
time: 77.2 us; the launch traced here: 76.9 us
  Pallas kernels  73.7 us (95%)
  local copies, waits for them, and re-layouts  2.62 us (3%)
    pallas_call x1, Pallas kernels, per_device(): pl.pallas_call(kernel, out_shape=(jax.ShapeDtypeStruct((GROUP, RIGHT), BF...  73.7 us
    unnamed x2, local copies, waits for them, and re-layouts  2.62 us

profile of v1, /device:TPU:8, one launch (start us, length us, event | category | flops | bytes accessed | tf_op | source)
XLA Modules:
  0.0 76.9 jit_solution(8032186453322556708)
XLA Ops:
  0.6 73.7 %shard_map.68 = (bf16[24,1024]{1,0:T(8,128)(2,1)}, f32[2,24]{1,0:T(2,128)}) custom-call(bf16[96,8,1024]{2,1,0:T(8,128)(2,1)} %bitcast.13, bf16[1024,8,128]{2,1,0:T(8,128)(2,1)} %bitcast.11, bf16[1024,8,128]{2,1,0:T(8,128)(2,1)} %bitcast.12, s32[2,768]{1,0:T(2,128)} %outcomes.1, s32[2,768]{1,0:T(2,128)} %basis.1), custom_call_target="tpu_custom_call" | custom-call | tf_op jit(solution)/shard_map/pallas_call | solution.py:443
  74.3 1.4 %copy.11 = bf16[24,1024]{1,0:T(8,128)(2,1)} copy(bf16[24,1024]{1,0:T(8,128)(2,1)} %get-tuple-element.4) | data formatting | bytes 98304
  75.7 1.2 %copy.12 = f32[2,24]{1,0:T(2,128)} copy(f32[2,24]{1,0:T(2,128)} %get-tuple-element.5) | data formatting | bytes 384

commit v2 on v1

v2 whole, which is shorter than its diff:
```python
import jax
import jax.numpy as jnp
from jax import lax
from jax.experimental import pallas as pl
from jax.experimental.pallas import tpu as pltpu
from jax.sharding import PartitionSpec as P

CHI = 16384
HALF_ROOT = 0.7071067811865476
F32 = jnp.float32
BF16 = jnp.bfloat16
MESH = pl.DeviceIdType.MESH

NA = 4
NZ = 16
G = NA * NA
HZ = NZ // 2
GROUP = 24
NB = 3
SB = GROUP // NB
R = 2 * SB
COLS = 512
RIGHT = 1024
NQ = 4
LW = 512 // NQ
RZ = 2 * GROUP


def coefficients(sel):
    rotated = sel >= 1.5
    odd = (sel == 1.0) | (sel == 3.0)
    sign = jnp.where(odd, -HALF_ROOT, HALF_ROOT)
    a = jnp.where(rotated, HALF_ROOT, jnp.where(odd, 0.0, 1.0))
    b = jnp.where(rotated, sign, jnp.where(odd, 1.0, 0.0))
    c = jnp.where(rotated, HALF_ROOT, jnp.where(odd, 1.0, 0.0))
    d = jnp.where(rotated, -sign, jnp.where(odd, 0.0, 1.0))
    return ((a, b), (c, d))


def kernel(
    env_hbm,
    te_hbm,
    to_hbm,
    outcomes_hbm,
    basis_hbm,
    out_ref,
    chosen_ref,
    both_ref,
    env_v,
    te_v,
    to_v,
    outcomes,
    basis,
    flat,
    w0,
    acc0,
    sel,
    s1,
    r1,
    s2,
    r2,
    r2o,
    g_buf,
    lhs,
    tb,
    acc1,
    part,
    zs,
    zr,
    fin,
    square,
    msg,
    n0r,
    nfs,
    nfr,
    load_sem,
    te_sem,
    s1_sem,
    r1_sem,
    s2_sem,
    s2o_sem,
    r2_sem,
    gb_ssem,
    gb_rsem,
    tb_ssem,
    tb_rsem,
    z_ssem,
    z_rsem,
    n0_ssem,
    n0_rsem,
    nf_ssem,
    nf_rsem,
    known,
):
    row = lax.axis_index("row")
    col = lax.axis_index("col")
    z = col // 2
    core = col % 2
    x = row % NA
    y = row // NA
    first_place = (x, y)
    second_place = (y, x)

    def at(px, py, pz, pc):
        return {"row": py * NA + px, "col": pz * 2 + pc}

    def peer(f, a, b, pc):
        return at(a, b, z, pc) if f == 0 else at(b, a, z, pc)

    def send(src, dst, ssem, rsem, device):
        pltpu.make_async_remote_copy(
            src_ref=src, dst_ref=dst, send_sem=ssem, recv_sem=rsem, device_id=device, device_id_type=MESH
        ).start()

    def wait_bytes(ref, sem):
        pltpu.make_async_copy(ref, ref, sem).wait()

    codes = [
        pltpu.make_async_copy(outcomes_hbm, outcomes, load_sem.at[0]),
        pltpu.make_async_copy(basis_hbm, basis, load_sem.at[1]),
    ]
    even = [
        pltpu.make_async_copy(te_hbm.at[pl.ds(i * 256, 256)], te_v.at[pl.ds(i * 256, 256)], te_sem.at[i])
        for i in range(4)
    ]
    vectors = pltpu.make_async_copy(env_hbm, env_v, load_sem.at[2])
    odd = pltpu.make_async_copy(to_hbm, to_v, load_sem.at[3])
    for load in (*even, *codes, vectors):
        load.start()

    barrier = pltpu.get_barrier_semaphore()

    def signal(sem, device):
        pl.semaphore_signal(sem, inc=1, device_id=device, device_id_type=MESH)

    for dc in range(2):
        if dc:
            signal(barrier, at(x, y, z, 1 - core))
        for d in range(1, NA):
            signal(barrier, at((x + d) % NA, y, z, (core + dc) % 2))
            signal(barrier, at(x, (y + d) % NA, z, (core + dc) % 2))
    for dz in (1, NZ - 1):
        signal(barrier, at(x, y, (z + dz) % NZ, core))

    def tell(i):
        for dz in (2**i, NZ - 2**i):
            signal(known.at[i], at(x, y, (z + dz) % NZ, core))

    def hear(i):
        pl.semaphore_wait(known.at[i], 2)

    for i in range(4):
        even[i].wait()
        for j in range(2):
            l0 = i * 256 + j * 128
            flat[j * 1024 : j * 1024 + 1024, :] = te_v[l0 : l0 + 128].astype(F32).reshape(1024, 128)
            for lt in range(4):
                for s in range(2):
                    lo = s * COLS + lt * 128
                    w0[l0 : l0 + 128, lo : lo + 128] = flat[
                        pl.ds(j * 1024 + lt * 2 + s, 128, stride=8), :
                    ].astype(BF16)
    odd.start()

    for load in codes:
        load.wait()
    eye = lax.broadcasted_iota(jnp.int32, (128, 128), 0) == lax.broadcasted_iota(jnp.int32, (128, 128), 1)
    for s in range(2):
        for j in range(6):
            lanes = slice(j * 128, (j + 1) * 128)
            code = (2 * basis[s : s + 1, lanes] + outcomes[s : s + 1, lanes]).astype(F32)
            column = jnp.sum(jnp.where(eye, jnp.broadcast_to(code, (128, 128)), 0.0), axis=1, keepdims=True)
            sel[s, j * 128 : (j + 1) * 128, :] = jnp.broadcast_to(column, (128, 128))
    vectors.wait()

    def multiply_first(k):
        rows = env_v[:, k].reshape(2 * G * SB, 1024)
        for n in range(2):
            acc0[k, :, n * 512 : n * 512 + 512] = jnp.dot(
                rows, w0[:, n * 512 : n * 512 + 512], preferred_element_type=F32
            )

    def build_first(k, v):
        def one(gp, carry):
            g = gp // 2
            p = gp % 2
            gx = g % NA
            gy = g // NA
            rows = pl.ds(pl.multiple_of(gp * SB, 8), SB)
            cu, cd = coefficients(sel[0, pl.ds(pl.multiple_of(gp * GROUP + k * SB, 8), SB), :])[v]
            for f in range(2):
                halves = []
                for h in range(2):
                    lo = h * 256 + f * 128
                    halves.append(
                        cu * acc0[k, rows, lo : lo + 128] + cd * acc0[k, rows, COLS + lo : COLS + lo + 128]
                    )
                ga, gb = (gx, gy) if f == 0 else (gy, gx)
                s1[k, v, f, p, ga, gb] = jnp.concatenate(halves, axis=0).astype(BF16)
            return carry

        lax.fori_loop(0, 2 * G, one, 0, unroll=4)

    def send_first(k, v):
        for da in (2, 1, 3, 0):
            for f in range(2):
                a = (first_place[f] + da) % NA
                for dc in range(2):
                    if da == 0 and dc == 0:
                        continue
                    pc = (core + dc) % 2
                    send(
                        s1.at[k, v, f, pc, a],
                        r1.at[k, v, f, first_place[f] * 2 + core],
                        s1_sem,
                        r1_sem.at[k, v, f],
                        peer(f, a, second_place[f], pc),
                    )

    def reduce_first(k, v):
        for f in range(2):
            r1[k, v, f, first_place[f] * 2 + core] = s1[k, v, f, core, first_place[f]]
            wait_bytes(r1.at[k, v, f, 0:7], r1_sem.at[k, v, f])
            for b in range(NA):
                for c in range(2):
                    total = r1[k, v, f, c, b].astype(F32)
                    for a in range(1, NA):
                        total = total + r1[k, v, f, a * 2 + c, b].astype(F32)
                    s2[k, v, f, b, c] = total.astype(BF16)
            for db in (2, 1, 3):
                b = (second_place[f] + db) % NA
                device = peer(f, first_place[f], b, core)
                if v == 0:
                    send(s2.at[k, v, f], r2.at[k, f, second_place[f]], s2_sem, r2_sem.at[k, v, f], device)
                else:
                    send(s2.at[k, v, f, b], r2o.at[k, f, second_place[f]], s2o_sem, r2_sem.at[k, v, f], device)

    lane = lax.broadcasted_iota(jnp.int32, (GROUP, 128), 1)
    sub = lax.broadcasted_iota(jnp.int32, (GROUP, 128), 0)

    def norms_to_lanes(squares, count, base):
        sums = jnp.sum(squares, axis=1, keepdims=True)
        column = sums[:count] + sums[count:]
        return jnp.sum(jnp.where(lane[:count] == sub[:count] + base, column, 0.0), axis=0, keepdims=True)

    def finish_chosen(k):
        squares = jnp.zeros((R, 128), F32)
        for f in range(2):
            r2[k, f, second_place[f]] = s2[k, 0, f]
            wait_bytes(r2.at[k, f, 0:3], r2_sem.at[k, 0, f])
            for b in range(NA):
                for c in range(2):
                    total = r2[k, f, 0, b, c].astype(F32)
                    for e in range(1, NA):
                        total = total + r2[k, f, e, b, c].astype(F32)
                    g_buf[k, f, first_place[f], b, c] = total.astype(BF16)
            for da in (2, 1, 3):
                a = (first_place[f] + da) % NA
                here = g_buf.at[k, f, first_place[f]]
                send(here, here, gb_ssem, gb_rsem.at[k, f], peer(f, a, second_place[f], core))
        for f in range(2):
            for c in range(2):
                total = r2[k, f, 0, second_place[f], c].astype(F32)
                for e in range(1, NA):
                    total = total + r2[k, f, e, second_place[f], c].astype(F32)
                squares = squares + total * total
        msg[0:1, :] += norms_to_lanes(squares, SB, 64 + k * SB)

    def finish_other(k):
        squares = jnp.zeros((R, 128), F32)
        for f in range(2):
            r2o[k, f, second_place[f]] = s2[k, 1, f, second_place[f]]
            wait_bytes(r2o.at[k, f, 0:3], r2_sem.at[k, 1, f])
            for c in range(2):
                total = r2o[k, f, 0, c].astype(F32)
                for e in range(1, NA):
                    total = total + r2o[k, f, e, c].astype(F32)
                squares = squares + total * total
        msg[0:1, :] += norms_to_lanes(squares, SB, 96 + k * SB)

    def gather_left(k):
        for f in range(2):
            wait_bytes(g_buf.at[k, f, 0:3], gb_rsem.at[k, f])

        def pair(j, carry):
            m0 = pl.multiple_of(k * G * SB + j * 2 * SB, 2 * SB)
            gy = j // 2
            for f in range(2):
                for c in range(2):
                    two = []
                    for e in range(2):
                        gx = (2 * j + e) % NA
                        ga, gb = (gx, gy) if f == 0 else (gy, gx)
                        two.append(g_buf[k, f, ga, gb, c].astype(F32))
                    for h in range(2):
                        lo = h * 512 + c * 256 + f * 128
                        lhs[pl.ds(m0, 2 * SB), lo : lo + 128] = jnp.concatenate(
                            [t[h * SB : (h + 1) * SB] for t in two], axis=0
                        ).astype(BF16)
            return carry

        lax.fori_loop(0, G // 2, pair, 0, unroll=2)

    def multiply_second(q):
        for n in range(4 * LW // 256):
            lo = q * 4 * LW + n * 256
            acc1[q, :, n * 256 : n * 256 + 256] = jnp.dot(
                lhs[...], tb[:, :, :, lo : lo + 256].reshape(1024, 256), preferred_element_type=F32
            )

        def one(g, carry):
            pairs = []
            for k in range(NB):
                samples = pl.ds(pl.multiple_of((2 * g + core) * GROUP + k * SB, 8), SB)
                pairs.append(coefficients(sel[1, samples, :]))
            for t in range(LW // 128):
                chunks = ([], [])
                for h in range(2):
                    for k in range(NB):
                        rows = pl.ds(pl.multiple_of(k * G * SB + g * SB, 8), SB)
                        lo = h * LW + t * 128
                        up = acc1[q, rows, lo : lo + 128]
                        down = acc1[q, rows, 2 * LW + lo : 2 * LW + lo + 128]
                        for v in range(2):
                            cu, cd = pairs[k][v]
                            chunks[v].append(cu * up + cd * down)
                for v in range(2):
                    part[v, q, g, :, t * 128 : t * 128 + 128] = jnp.concatenate(chunks[v], axis=0).astype(BF16)
            return carry

        lax.fori_loop(0, G, one, 0, unroll=2)

    def hops(v, d):
        return HZ - v if d == 0 else HZ - 1 + v

    def slot(v, d, s):
        return {(0, 0): 0, (0, 1): HZ, (1, 0): 2 * HZ - 1, (1, 1): 3 * HZ - 2}[v, d] + s

    def ring_step(q, s):
        for v in range(2):
            for d in range(2):
                n = hops(v, d)
                if s >= n:
                    continue
                owner = (z + n - s) % NZ if d == 0 else (z + NZ - n + s) % NZ
                step = 1 if d == 0 else NZ - 1
                here = slot(v, d, s)
                if s == 0:
                    src = part.at[v, q, owner]
                else:
                    wait_bytes(zr.at[q, here - 1], z_rsem.at[q, here - 1])
                    zs[q, here] = (zr[q, here - 1].astype(F32) + part[v, q, owner].astype(F32)).astype(BF16)
                    src = zs.at[q, here]
                send(src, zr.at[q, here], z_ssem, z_rsem.at[q, here], at(x, y, (z + step) % NZ, core))

    def ring_end(q):
        for v in range(2):
            total = part[v, q, z].astype(F32)
            for d in range(2):
                last = slot(v, d, hops(v, d) - 1)
                wait_bytes(zr.at[q, last], z_rsem.at[q, last])
                total = total + zr[q, last].astype(F32)
            if v == 0:
                for h in range(2):
                    fin[:, h * 512 + q * LW : h * 512 + q * LW + LW] = total[h * GROUP : (h + 1) * GROUP]
            squares = total[:, 0:128] * total[:, 0:128]
            for t in range(1, LW // 128):
                squares = squares + total[:, t * 128 : t * 128 + 128] * total[:, t * 128 : t * 128 + 128]
            square[v] = squares if q == 0 else square[v] + squares

    msg[...] = jnp.zeros_like(msg)
    for k in range(NB):
        multiply_first(k)
        build_first(k, 0)
        if k == 0:
            pl.semaphore_wait(barrier, 15)
            tell(0)
        send_first(k, 0)

    odd.wait()

    def spread_odd(i, carry):
        flat[...] = to_v[pl.ds(i * 256, 256)].astype(F32).reshape(2048, 128)
        h = i // 2
        w = pl.multiple_of((i % 2) * 128, 128)
        for lt in range(8):
            for s in range(2):
                within = (lt % 4) * 128
                lo = (within // LW) * 4 * LW + s * 2 * LW + (lt // 4) * LW + within % LW
                tb[h, core, pl.ds(w, 128), lo : lo + 128] = flat[pl.ds(lt * 2 + s, 128, stride=16), :].astype(BF16)
        return carry

    lax.fori_loop(0, 2, spread_odd, 0)
    reduce_first(0, 0)
    lax.fori_loop(2, 4, spread_odd, 0)
    for h in range(2):
        send(tb.at[h, core], tb.at[h, core], tb_ssem, tb_rsem, at(x, y, z, 1 - core))
    hear(0)
    tell(1)
    reduce_first(1, 0)
    reduce_first(2, 0)
    for k in range(NB):
        build_first(k, 1)
    hear(1)
    tell(2)
    for k in range(NB):
        finish_chosen(k)
    for k in range(NB):
        send_first(k, 1)
    hear(2)
    wait_bytes(tb.at[:, 0], tb_rsem)
    for k in range(NB):
        gather_left(k)
    for q in range(NQ):
        multiply_second(q)
        ring_step(q, 0)
    for s in range(1, HZ):
        for q in range(NQ):
            ring_step(q, s)
        if s == 2:
            for k in range(NB):
                reduce_first(k, 1)
        if s == 4:
            for k in range(NB):
                finish_other(k)
            n0r[z] = msg[0:1, :]
            nfs[0:1, :] = msg[0:1, :]

            @pl.when(z != row)
            def _():
                send(nfs.at[0:1], n0r.at[z], n0_ssem, n0_rsem, at(x, y, row, core))

    for q in range(NQ):
        ring_end(q)

    own = norms_to_lanes(square[0], GROUP, 0) + norms_to_lanes(square[1], GROUP, 32)
    nfs[1:2, :] = own

    @pl.when(z == row)
    def _():
        wait_bytes(n0r.at[0 : NZ - 1], n0_rsem)
        nfs[1:2, :] = own + jnp.sum(n0r[...], axis=0)

    nfr[row] = nfs[1:2, :]
    for dx in (2, 1, 3, 0):
        for dy in (2, 1, 3, 0):
            if dx or dy:
                send(nfs.at[1:2], nfr.at[row], nf_ssem, nf_rsem, at((x + dx) % NA, (y + dy) % NA, z, core))

    wait_bytes(r1.at[:, :, :, 0:7], s1_sem)
    wait_bytes(r2.at[:, :, 0:3], s2_sem)
    wait_bytes(r2o.at[:, :, 0:3], s2o_sem)
    wait_bytes(g_buf.at[:, :, 0:3], gb_ssem)
    wait_bytes(tb.at[:, 0], tb_ssem)
    wait_bytes(zr, z_ssem)

    @pl.when(z != row)
    def _():
        wait_bytes(n0r.at[0], n0_ssem)

    wait_bytes(nfr.at[0 : G - 1], nf_rsem)
    norms = jnp.sum(nfr[...], axis=0)
    both = norms + pltpu.roll(norms, 96, 1)
    chosen_ref[0:1, :] = pltpu.roll(norms, 64, 1)[:, :GROUP]
    chosen_ref[1:2, :] = norms[:, :GROUP]
    both_ref[0:1, :] = pltpu.roll(both, 64, 1)[:, :GROUP]
    both_ref[1:2, :] = both[:, :GROUP]
    column = jnp.sum(jnp.where(lane == sub, jnp.broadcast_to(norms, (GROUP, 128)), 0.0), axis=1, keepdims=True)
    out_ref[...] = fin[...] * jnp.sqrt(CHI / column)
    wait_bytes(nfr.at[0 : G - 1], nf_ssem)


def per_device(environment, even_site, odd_site, outcomes, basis_codes):
    samples, left = environment.shape
    env = environment.reshape(2 * G, NB, SB, left)
    te = even_site.reshape(left, 2, 4, 128).transpose(0, 2, 1, 3).reshape(left, 8, 128)
    to = odd_site.reshape(512, 2, 8, 128).transpose(0, 2, 1, 3).reshape(1024, 8, 128)
    vmem = pl.BlockSpec(memory_space=pltpu.VMEM)
    hbm = pl.BlockSpec(memory_space=pl.ANY)
    dma = pltpu.SemaphoreType.DMA
    nz_slots = 4 * HZ - 2
    final, chosen_norms, both_norms = pl.pallas_call(
        kernel,
        out_shape=(
            jax.ShapeDtypeStruct((GROUP, RIGHT), F32),
            jax.ShapeDtypeStruct((2, GROUP), F32),
            jax.ShapeDtypeStruct((2, GROUP), F32),
        ),
        in_specs=[hbm] * 5,
        out_specs=(vmem,) * 3,
        scratch_shapes=[
            pltpu.VMEM((2 * G, NB, SB, left), BF16),
            pltpu.VMEM((left, 8, 128), BF16),
            pltpu.VMEM((1024, 8, 128), BF16),
            pltpu.VMEM((2, samples), jnp.int32),
            pltpu.VMEM((2, samples), jnp.int32),
            pltpu.VMEM((2048, 128), F32),
            pltpu.VMEM((left, 2 * COLS), BF16),
            pltpu.VMEM((NB, 2 * G * SB, 2 * COLS), F32),
            pltpu.VMEM((2, samples, 128), F32),
            pltpu.VMEM((NB, 2, 2, 2, NA, NA, R, 128), BF16),
            pltpu.VMEM((NB, 2, 2, 2 * NA, NA, R, 128), BF16),
            pltpu.VMEM((NB, 2, 2, NA, 2, R, 128), BF16),
            pltpu.VMEM((NB, 2, NA, NA, 2, R, 128), BF16),
            pltpu.VMEM((NB, 2, NA, 2, R, 128), BF16),
            pltpu.VMEM((NB, 2, NA, NA, 2, R, 128), BF16),
            pltpu.VMEM((NB * G * SB, 1024), BF16),
            pltpu.VMEM((2, 2, 256, 2 * RIGHT), BF16),
            pltpu.VMEM((NQ, NB * G * SB, 4 * LW), F32),
            pltpu.VMEM((2, NQ, NZ, RZ, LW), BF16),
            pltpu.VMEM((NQ, nz_slots, RZ, LW), BF16),
            pltpu.VMEM((NQ, nz_slots, RZ, LW), BF16),
            pltpu.VMEM((GROUP, RIGHT), F32),
            pltpu.VMEM((2, RZ, 128), F32),
            pltpu.VMEM((8, 128), F32),
            pltpu.VMEM((NZ, 1, 128), F32),
            pltpu.VMEM((8, 128), F32),
            pltpu.VMEM((G, 1, 128), F32),
            dma((4,)),
            dma((4,)),
            dma,
            dma((NB, 2, 2)),
            dma,
            dma,
            dma((NB, 2, 2)),
            dma,
            dma((NB, 2)),
            dma,
            dma,
            dma,
            dma((NQ, nz_slots)),
            dma,
            dma,
            dma,
            dma,
            pltpu.SemaphoreType.REGULAR((3,)),
        ],
        compiler_params=pltpu.CompilerParams(
            collective_id=0, has_side_effects=True, vmem_limit_bytes=60 * 1024 * 1024
        ),
    )(env, te, to, outcomes, basis_codes)
    return final.astype(BF16), chosen_norms / both_norms


def solution(mesh):
    placed = (P(None, "row"), P("row", None, "col"), P("col", None, "row"), P(), P())
    return jax.shard_map(
        per_device,
        mesh=mesh,
        in_specs=placed,
        out_specs=(P("col", "row"), P(None, "col")),
        check_vma=False,
    )
```

time: 77.2 us -> 68.9 us (0.89)
  Pallas kernels: 73.7 us -> 65.4 us
  other arithmetic: 0 us -> 2.77 us
  local copies, waits for them, and re-layouts: 2.62 us -> 0 us
    pallas_call x1, Pallas kernels: 73.7 us -> 65.4 us  [per_device(): pl.pallas_call(kernel, out_shape=(jax.ShapeDtypeStruct((GROUP, RIGHT), F3...]
    unnamed x2 -> x0, local copies, waits for them, and re-layouts: 2.62 us -> none
    convert_element_type x0 -> x1, other arithmetic: none -> 1.52 us  [per_device(): return (final.astype(BF16), chosen_norms / both_norms)]
    div x0 -> x1, other arithmetic: none -> 1.25 us  [per_device(): return (final.astype(BF16), chosen_norms / both_norms)]
where the time goes in v2:
time: 68.9 us; the launch traced here: 68.8 us
  Pallas kernels  65.4 us (95%)
  other arithmetic  2.77 us (4%)
    pallas_call x1, Pallas kernels, per_device(): pl.pallas_call(kernel, out_shape=(jax.ShapeDtypeStruct((GROUP, RIGHT), F3...  65.4 us
    convert_element_type x1, other arithmetic, per_device(): return (final.astype(BF16), chosen_norms / both_norms)  1.52 us

profile of v2, /device:TPU:8, one launch (start us, length us, event | category | flops | bytes accessed | tf_op | source)
XLA Modules:
  0.0 68.8 jit_solution(14149798666360914071)
XLA Ops:
  0.6 65.4 %shard_map.68 = (f32[24,1024]{1,0:T(8,128)}, f32[2,24]{1,0:T(2,128)}, f32[2,24]{1,0:T(2,128)}) custom-call(bf16[32,3,8,1024]{3,2,1,0:T(8,128)(2,1)} %bitcast.13, bf16[1024,8,128]{2,1,0:T(8,128)(2,1)} %bitcast.11, bf16[1024,8,128]{2,1,0:T(8,128)(2,1)} %bitcast.12, s32[2,768]{1,0:T(2,128)} %outcomes_hbm.1, s32[2,768]{1,0:T(2,128)} %basis_hbm.1), custom_call_target="tpu_custom_call" | custom-call | tf_op jit(solution)/shard_map/pallas_call | solution.py:482
  66.0 1.3 %div.3 = f32[2,24]{1,0:T(2,128)} divide(f32[2,24]{1,0:T(2,128)} %get-tuple-element.6, f32[2,24]{1,0:T(2,128)} %get-tuple-element.7) | non-fusion elementwise | flops 48 | bytes 576 | tf_op jit(solution)/shard_map/div | solution.py:542
  67.3 1.5 %convert_element_type.3 = bf16[24,1024]{1,0:T(8,128)(2,1)} convert(f32[24,1024]{1,0:T(8,128)} %get-tuple-element.5) | non-fusion elementwise | flops 24576 | bytes 147456 | tf_op jit(solution)/shard_map/convert_element_type | solution.py:542

commit v3 on v2

--- a/solution.py
+++ b/solution.py
@@ -24,6 +24,7 @@
 NQ = 4
 LW = 512 // NQ
 RZ = 2 * GROUP
+AHEAD = True
 
 
 def coefficients(sel):
@@ -67,6 +68,8 @@
     part,
     zs,
     zr,
+    cf,
+    mine,
     fin,
     square,
     msg,
@@ -86,6 +89,8 @@
     tb_rsem,
     z_ssem,
     z_rsem,
+    m_ssem,
+    m_rsem,
     n0_ssem,
     n0_rsem,
     nf_ssem,
@@ -98,6 +103,7 @@
     core = col % 2
     x = row % NA
     y = row // NA
+    par = (core + z) % 2
     first_place = (x, y)
     second_place = (y, x)
 
@@ -125,7 +131,7 @@
     ]
     vectors = pltpu.make_async_copy(env_hbm, env_v, load_sem.at[2])
     odd = pltpu.make_async_copy(to_hbm, to_v, load_sem.at[3])
-    for load in (*even, *codes, vectors):
+    for load in (*codes, *even, vectors):
         load.start()
 
     barrier = pltpu.get_barrier_semaphore()
@@ -139,15 +145,26 @@
         for d in range(1, NA):
             signal(barrier, at((x + d) % NA, y, z, (core + dc) % 2))
             signal(barrier, at(x, (y + d) % NA, z, (core + dc) % 2))
-    for dz in (1, NZ - 1):
-        signal(barrier, at(x, y, (z + dz) % NZ, core))
+        for dz in (1, NZ - 1):
+            signal(barrier, at(x, y, (z + dz) % NZ, (core + dc) % 2))
 
     def tell(i):
         for dz in (2**i, NZ - 2**i):
-            signal(known.at[i], at(x, y, (z + dz) % NZ, core))
+            for dc in range(2):
+                signal(known.at[i], at(x, y, (z + dz) % NZ, (core + dc) % 2))
 
     def hear(i):
-        pl.semaphore_wait(known.at[i], 2)
+        pl.semaphore_wait(known.at[i], 4)
+
+    for load in codes:
+        load.wait()
+    eye = lax.broadcasted_iota(jnp.int32, (128, 128), 0) == lax.broadcasted_iota(jnp.int32, (128, 128), 1)
+    for s in range(2):
+        for j in range(6):
+            lanes = slice(j * 128, (j + 1) * 128)
+            code = (2 * basis[s : s + 1, lanes] + outcomes[s : s + 1, lanes]).astype(F32)
+            column = jnp.sum(jnp.where(eye, jnp.broadcast_to(code, (128, 128)), 0.0), axis=1, keepdims=True)
+            sel[s, j * 128 : (j + 1) * 128, :] = jnp.broadcast_to(column, (128, 128))
 
     for i in range(4):
         even[i].wait()
@@ -162,15 +179,6 @@
                     ].astype(BF16)
     odd.start()
 
-    for load in codes:
-        load.wait()
-    eye = lax.broadcasted_iota(jnp.int32, (128, 128), 0) == lax.broadcasted_iota(jnp.int32, (128, 128), 1)
-    for s in range(2):
-        for j in range(6):
-            lanes = slice(j * 128, (j + 1) * 128)
-            code = (2 * basis[s : s + 1, lanes] + outcomes[s : s + 1, lanes]).astype(F32)
-            column = jnp.sum(jnp.where(eye, jnp.broadcast_to(code, (128, 128)), 0.0), axis=1, keepdims=True)
-            sel[s, j * 128 : (j + 1) * 128, :] = jnp.broadcast_to(column, (128, 128))
     vectors.wait()
 
     def multiply_first(k):
@@ -181,13 +189,11 @@
             )
 
     def build_first(k, v):
-        def one(gp, carry):
-            g = gp // 2
-            p = gp % 2
-            gx = g % NA
-            gy = g // NA
-            rows = pl.ds(pl.multiple_of(gp * SB, 8), SB)
-            cu, cd = coefficients(sel[0, pl.ds(pl.multiple_of(gp * GROUP + k * SB, 8), SB), :])[v]
+        for gp in range(2 * G):
+            g, p = gp // 2, gp % 2
+            gx, gy = g % NA, g // NA
+            rows = slice(gp * SB, gp * SB + SB)
+            cu, cd = coefficients(sel[0, gp * GROUP + k * SB : gp * GROUP + k * SB + SB, :])[v]
             for f in range(2):
                 halves = []
                 for h in range(2):
@@ -197,9 +203,6 @@
                     )
                 ga, gb = (gx, gy) if f == 0 else (gy, gx)
                 s1[k, v, f, p, ga, gb] = jnp.concatenate(halves, axis=0).astype(BF16)
-            return carry
-
-        lax.fori_loop(0, 2 * G, one, 0, unroll=4)
 
     def send_first(k, v):
         for da in (2, 1, 3, 0):
@@ -210,7 +213,7 @@
                         continue
                     pc = (core + dc) % 2
                     send(
-                        s1.at[k, v, f, pc, a],
+                        s1.at[k, v, f, (pc + z) % 2, a],
                         r1.at[k, v, f, first_place[f] * 2 + core],
                         s1_sem,
                         r1_sem.at[k, v, f],
@@ -219,7 +222,7 @@
 
     def reduce_first(k, v):
         for f in range(2):
-            r1[k, v, f, first_place[f] * 2 + core] = s1[k, v, f, core, first_place[f]]
+            r1[k, v, f, first_place[f] * 2 + core] = s1[k, v, f, par, first_place[f]]
             wait_bytes(r1.at[k, v, f, 0:7], r1_sem.at[k, v, f])
             for b in range(NA):
                 for c in range(2):
@@ -301,6 +304,15 @@
 
         lax.fori_loop(0, G // 2, pair, 0, unroll=2)
 
+    def second_coefficients():
+        for k in range(NB):
+            for g in range(G):
+                samples = pl.ds(pl.multiple_of((2 * g + par) * GROUP + k * SB, 8), SB)
+                pairs = coefficients(sel[1, samples, :])
+                for v in range(2):
+                    for e in range(2):
+                        cf[v, e, (k * G + g) * SB : (k * G + g) * SB + SB, :] = pairs[v][e]
+
     def multiply_second(q):
         for n in range(4 * LW // 256):
             lo = q * 4 * LW + n * 256
@@ -308,27 +320,30 @@
                 lhs[...], tb[:, :, :, lo : lo + 256].reshape(1024, 256), preferred_element_type=F32
             )
 
-        def one(g, carry):
-            pairs = []
-            for k in range(NB):
-                samples = pl.ds(pl.multiple_of((2 * g + core) * GROUP + k * SB, 8), SB)
-                pairs.append(coefficients(sel[1, samples, :]))
+    def build_second(q):
+        for g in range(G):
             for t in range(LW // 128):
                 chunks = ([], [])
                 for h in range(2):
                     for k in range(NB):
-                        rows = pl.ds(pl.multiple_of(k * G * SB + g * SB, 8), SB)
+                        rows = slice((k * G + g) * SB, (k * G + g) * SB + SB)
                         lo = h * LW + t * 128
                         up = acc1[q, rows, lo : lo + 128]
                         down = acc1[q, rows, 2 * LW + lo : 2 * LW + lo + 128]
                         for v in range(2):
-                            cu, cd = pairs[k][v]
-                            chunks[v].append(cu * up + cd * down)
+                            chunks[v].append(cf[v, 0, rows, :] * up + cf[v, 1, rows, :] * down)
                 for v in range(2):
                     part[v, q, g, :, t * 128 : t * 128 + 128] = jnp.concatenate(chunks[v], axis=0).astype(BF16)
-            return carry
-
-        lax.fori_loop(0, G, one, 0, unroll=2)
+
+    def own_part(q):
+        @pl.when(z % 2 == 0)
+        def _():
+            mine[:, q] = part[:, q, z]
+
+        @pl.when(z % 2 == 1)
+        def _():
+            for v in range(2):
+                send(part.at[v, q, z], mine.at[v, q], m_ssem, m_rsem.at[q], at(x, y, z, 1 - core))
 
     def hops(v, d):
         return HZ - v if d == 0 else HZ - 1 + v
@@ -351,11 +366,16 @@
                     wait_bytes(zr.at[q, here - 1], z_rsem.at[q, here - 1])
                     zs[q, here] = (zr[q, here - 1].astype(F32) + part[v, q, owner].astype(F32)).astype(BF16)
                     src = zs.at[q, here]
-                send(src, zr.at[q, here], z_ssem, z_rsem.at[q, here], at(x, y, (z + step) % NZ, core))
+                target = par if s == n - 1 else 1 - core
+                send(src, zr.at[q, here], z_ssem, z_rsem.at[q, here], at(x, y, (z + step) % NZ, target))
 
     def ring_end(q):
+        @pl.when(z % 2 == 1)
+        def _():
+            wait_bytes(mine.at[:, q], m_rsem.at[q])
+
         for v in range(2):
-            total = part[v, q, z].astype(F32)
+            total = mine[v, q].astype(F32)
             for d in range(2):
                 last = slot(v, d, hops(v, d) - 1)
                 wait_bytes(zr.at[q, last], z_rsem.at[q, last])
@@ -368,12 +388,13 @@
                 squares = squares + total[:, t * 128 : t * 128 + 128] * total[:, t * 128 : t * 128 + 128]
             square[v] = squares if q == 0 else square[v] + squares
 
+    given_here = (z == row) & (par == core)
     msg[...] = jnp.zeros_like(msg)
     for k in range(NB):
         multiply_first(k)
         build_first(k, 0)
         if k == 0:
-            pl.semaphore_wait(barrier, 15)
+            pl.semaphore_wait(barrier, 17)
             tell(0)
         send_first(k, 0)
 
@@ -395,27 +416,37 @@
     lax.fori_loop(2, 4, spread_odd, 0)
     for h in range(2):
         send(tb.at[h, core], tb.at[h, core], tb_ssem, tb_rsem, at(x, y, z, 1 - core))
+    reduce_first(1, 0)
     hear(0)
     tell(1)
-    reduce_first(1, 0)
     reduce_first(2, 0)
-    for k in range(NB):
-        build_first(k, 1)
+    finish_chosen(0)
+    build_first(0, 1)
+    build_first(1, 1)
+    finish_chosen(1)
     hear(1)
     tell(2)
-    for k in range(NB):
-        finish_chosen(k)
+    build_first(2, 1)
+    finish_chosen(2)
     for k in range(NB):
         send_first(k, 1)
+    second_coefficients()
     hear(2)
     wait_bytes(tb.at[:, 0], tb_rsem)
     for k in range(NB):
         gather_left(k)
+    multiply_second(0)
     for q in range(NQ):
-        multiply_second(q)
+        if AHEAD and q + 1 < NQ:
+            multiply_second(q + 1)
+        build_second(q)
         ring_step(q, 0)
+        if not AHEAD and q + 1 < NQ:
+            multiply_second(q + 1)
     for s in range(1, HZ):
         for q in range(NQ):
+            if s == 1:
+                own_part(q)
             ring_step(q, s)
         if s == 2:
             for k in range(NB):
@@ -423,12 +454,15 @@
         if s == 4:
             for k in range(NB):
                 finish_other(k)
-            n0r[z] = msg[0:1, :]
             nfs[0:1, :] = msg[0:1, :]
 
-            @pl.when(z != row)
+            @pl.when(given_here)
             def _():
-                send(nfs.at[0:1], n0r.at[z], n0_ssem, n0_rsem, at(x, y, row, core))
+                n0r[z] = msg[0:1, :]
+
+            @pl.when(jnp.logical_not(given_here))
+            def _():
+                send(nfs.at[0:1], n0r.at[z], n0_ssem, n0_rsem, at(x, y, row, par))
 
     for q in range(NQ):
         ring_end(q)
@@ -436,9 +470,16 @@
     own = norms_to_lanes(square[0], GROUP, 0) + norms_to_lanes(square[1], GROUP, 32)
     nfs[1:2, :] = own
 
+    @pl.when(given_here)
+    def _():
+        wait_bytes(n0r.at[0 : NZ - 1], n0_rsem)
+
+    @pl.when((z == row) & (par != core))
+    def _():
+        wait_bytes(n0r, n0_rsem)
+
     @pl.when(z == row)
     def _():
-        wait_bytes(n0r.at[0 : NZ - 1], n0_rsem)
         nfs[1:2, :] = own + jnp.sum(n0r[...], axis=0)
 
     nfr[row] = nfs[1:2, :]
@@ -454,9 +495,13 @@
     wait_bytes(tb.at[:, 0], tb_ssem)
     wait_bytes(zr, z_ssem)
 
-    @pl.when(z != row)
+    @pl.when(jnp.logical_not(given_here))
     def _():
         wait_bytes(n0r.at[0], n0_ssem)
+
+    @pl.when(z % 2 == 1)
+    def _():
+        wait_bytes(mine, m_ssem)
 
     wait_bytes(nfr.at[0 : G - 1], nf_rsem)
     norms = jnp.sum(nfr[...], axis=0)
@@ -482,9 +527,9 @@
     final, chosen_norms, both_norms = pl.pallas_call(
         kernel,
         out_shape=(
-            jax.ShapeDtypeStruct((GROUP, RIGHT), F32),
-            jax.ShapeDtypeStruct((2, GROUP), F32),
-            jax.ShapeDtypeStruct((2, GROUP), F32),
+            pltpu.VMEM((GROUP, RIGHT), F32),
+            pltpu.VMEM((2, GROUP), F32),
+            pltpu.VMEM((2, GROUP), F32),
         ),
         in_specs=[hbm] * 5,
         out_specs=(vmem,) * 3,
@@ -510,6 +555,8 @@
             pltpu.VMEM((2, NQ, NZ, RZ, LW), BF16),
             pltpu.VMEM((NQ, nz_slots, RZ, LW), BF16),
             pltpu.VMEM((NQ, nz_slots, RZ, LW), BF16),
+            pltpu.VMEM((2, 2, NB * G * SB, 128), F32),
+            pltpu.VMEM((2, NQ, RZ, LW), BF16),
             pltpu.VMEM((GROUP, RIGHT), F32),
             pltpu.VMEM((2, RZ, 128), F32),
             pltpu.VMEM((8, 128), F32),
@@ -529,6 +576,8 @@
             dma,
             dma,
             dma((NQ, nz_slots)),
+            dma,
+            dma((NQ,)),
             dma,
             dma,
             dma,

time: 68.9 us -> 63.9 us (0.927)
  the two profiles are of different devices: /device:TPU:8 before, /device:TPU:1 now
where the time goes in v3:
time: 63.9 us; the launch traced here: 63.8 us
  Pallas kernels  61.9 us (97%)
  other arithmetic  1.2 us (2%)
  between operations  0.64 us (1%)
    pallas_call x1, Pallas kernels, per_device(): pl.pallas_call(kernel, out_shape=(pltpu.VMEM((GROUP, RIGHT), F32), pltpu....  61.9 us

profile of v3, /device:TPU:1, one launch (start us, length us, event | category | flops | bytes accessed | tf_op | source)
XLA Modules:
  0.0 63.8 jit_solution(12057866267610767317)
XLA Ops:
  0.6 61.9 %shard_map.68 = (f32[24,1024]{1,0:T(8,128)S(1)}, f32[2,24]{1,0:T(2,128)S(1)}, f32[2,24]{1,0:T(2,128)S(1)}) custom-call(bf16[32,3,8,1024]{3,2,1,0:T(8,128)(2,1)} %bitcast.13, bf16[1024,8,128]{2,1,0:T(8,128)(2,1)} %bitcast.11, bf16[1024,8,128]{2,1,0:T(8,128)(2,1)} %bitcast.12, s32[2,768]{1,0:T(2,128)} %outcomes_hbm.1, s32[2,768]{1,0:T(2,128)} %basis_hbm.1), custom_call_target="tpu_custom_call" | custom-call | tf_op jit(solution)/shard_map/pallas_call | solution.py:527
  62.6 0.6 div.3
  63.1 0.6 convert_element_type.3
